TPU v7x, 32 devices: a whole 2x2x4 slice. The times are simulated.
32 devices in a mesh: grp: 2 (over x), lat: 16 (over z, y, core).
Axes of the slice: x: 2, y: 2, z: 4, core: 2. Of those that a mesh axis runs over, the one named last changes fastest.
Arguments:
- acts: bfloat16 [128, 2, 2048], P(('grp', 'lat')), parts along dimension 0, may hold values from -6 to 6
- enc_weight: bfloat16 [4, 2048, 4096], P('grp', None, 'lat'), parts along dimension 0, may hold values from -0.09375 to 0.09375
- enc_bias: float32 [8192], P(('grp', 'lat')), parts along dimension 0, may hold values from -3 to 3
- dec_weight: bfloat16 [4096, 4, 2048], P('lat', 'grp'), parts along dimension 1, may hold values from -0.125 to 0.125
- dec_bias: float32 [4, 2048], P('grp'), parts along dimension 0, may hold values from -5 to 5
Outputs:
- residual: bfloat16 [128, 2, 2048], P(('grp', 'lat')), parts along dimension 0
- grad_enc: bfloat16 [4, 2048, 4096], P('grp', None, 'lat'), parts along dimension 0
- grad_enc_bias: float32 [8192], P(('grp', 'lat')), parts along dimension 0
- grad_dec: bfloat16 [4096, 4, 2048], P('lat', 'grp'), parts along dimension 1
- grad_dec_bias: float32 [4, 2048], P('grp'), parts along dimension 0
There are 2 independent parts, one for each index of `grp`. A program takes and returns all parts, laid end to end along the dimension named above; each array names one. Nothing has to cross between parts.
All inputs are finite; a program needn't handle non-finite values.
Results may differ from a plain program's by a relative error of at most 0.015.
Values may be sent and summed in bfloat16 or wider, within the bound.
No kernel may reach another device: no remote copies, remote signals or barrier semaphores. Data moves between devices by JAX's collectives and lax.ppermute only.
A program may use at most 128 MiB of HBM per device.

v0:
```python
import jax
import jax.numpy as jnp
from jax import lax
from jax.sharding import PartitionSpec as P

sparsity_weight = 2.0


def body(acts, enc_weight, enc_bias, dec_weight, dec_bias):
    tok_dev, layers, width = acts.shape
    lat_dev = enc_weight.shape[2]
    wide = layers * width
    total_rows = tok_dev * lax.axis_size("lat")
    factor = 2.0 / total_rows
    flat_rows = acts.reshape(tok_dev, wide)
    flat_enc = enc_weight.reshape(wide, lat_dev)
    flat_dec = dec_weight.reshape(lat_dev, wide)
    flat_bias = dec_bias.reshape(wide)
    own_start = lax.axis_index("lat") * tok_dev
    gathered = lax.all_gather(flat_rows, "lat", axis=0, tiled=True)
    before = jnp.dot(gathered, flat_enc, preferred_element_type=jnp.float32) + enc_bias
    active = jnp.maximum(before, 0.0).astype(jnp.bfloat16)
    dec_wide = dec_weight.astype(jnp.float32)
    row_sq = jnp.sum(dec_wide * dec_wide, axis=2)
    inv_norm = lax.rsqrt(row_sq + 1.0)
    dec_norm = jnp.sum(jnp.sqrt(row_sq + 1.0), axis=1)
    term = jnp.dot(active, flat_dec, preferred_element_type=jnp.float32)
    own_term = lax.dynamic_slice_in_dim(term, own_start, tok_dev, 0)
    own_term = own_term + flat_bias - flat_rows.astype(jnp.float32)
    term = lax.dynamic_update_slice_in_dim(term, own_term, own_start, 0)
    summed = lax.psum(term, "lat")
    all_residual = summed.astype(jnp.bfloat16)
    own_residual = lax.dynamic_slice_in_dim(all_residual, own_start, tok_dev, 0)
    grad_dec_bias = factor * jnp.sum(all_residual.astype(jnp.float32), axis=0)
    dec_total = lax.dot_general(
        active, all_residual, (((0,), (0,)), ((), ())), preferred_element_type=jnp.float32
    )
    backward = lax.dot_general(
        all_residual, flat_dec, (((1,), (1,)), ((), ())), preferred_element_type=jnp.float32
    )
    grad_act = factor * backward + sparsity_weight / total_rows * dec_norm
    grad_before = jnp.where(before > 0.0, grad_act, 0.0).astype(jnp.bfloat16)
    enc_total = lax.dot_general(
        gathered, grad_before, (((0,), (0,)), ((), ())), preferred_element_type=jnp.float32
    )
    grad_enc = enc_total.astype(jnp.bfloat16).reshape(layers, width, lat_dev)
    grad_enc_bias = jnp.sum(grad_before.astype(jnp.float32), axis=0)
    act_sum = jnp.sum(active.astype(jnp.float32), axis=0)
    grad_dec = (
        factor * dec_total.reshape(lat_dev, layers, width)
        + sparsity_weight / total_rows * act_sum[:, None, None] * dec_wide * inv_norm[:, :, None]
    ).astype(jnp.bfloat16)
    return (
        own_residual.reshape(tok_dev, layers, width),
        grad_enc,
        grad_enc_bias,
        grad_dec,
        grad_dec_bias.reshape(layers, width),
    )


def solution(mesh):
    return jax.shard_map(
        body,
        mesh=mesh,
        in_specs=(
            P(("grp", "lat"), None, None),
            P("grp", None, "lat"),
            P(("grp", "lat")),
            P("lat", "grp", None),
            P("grp", None),
        ),
        out_specs=(
            P(("grp", "lat"), None, None),
            P("grp", None, "lat"),
            P(("grp", "lat")),
            P("lat", "grp", None),
            P("grp", None),
        ),
        check_vma=False,
    )
```

profile of v0, /device:TPU:0, one launch (start us, length us, event | category | flops | bytes accessed | tf_op | source)
XLA Modules:
  0.0 136.5 jit_solution(2590079693091624209)
XLA Ops:
  0.6 0.0 copy-start
  0.7 1.6 %copy-done = bf16[2,2048,256]{2,1,0:T(8,128)(2,1)S(1)} copy-done((bf16[2,2048,256]{2,1,0:T(8,128)(2,1)S(1)}, bf16[2,2048,256]{2,1,0:T(8,128)(2,1)}, u32[]{:S(2)}) %copy-start) | copy-done | bytes 2097176
  2.2 0.7 copy.14
  2.9 0.8 reshape.50
  3.7 0.8 convert_bitcast_fusion
  4.5 0.0 copy-start.3
  4.6 3.8 %fusion.1 = f32[256,2]{1,0:T(8,128)S(1)} fusion(bf16[256,2,2048]{2,1,0:T(2,128)(2,1)} %param.8), kind=kLoop, calls=%fused_computation.5 | loop fusion | flops 3145216 | bytes 2099200 | tf_op jit(solution)/shard_map/reduce_sum | solution.py:24
  8.4 0.1 add_rsqrt_fusion
  8.6 24.6 %all-gather = bf16[16,4,4096]{2,1,0:T(4,128)(2,1)S(1)} all-gather(bf16[1,4,4096]{2,1,0:T(4,128)(2,1)S(1)} %reshape.50), channel_id=1, replica_groups=mesh['grp'=2,'lat'=16] {'lat'}, dimensions={0}, use_global_device_ids=true | all-gather | bytes 557056 | tf_op jit(solution)/shard_map/all_gather | solution.py:20
  33.2 0.1 reshape.51
  33.3 0.0 copy-done.3
  33.3 0.0 copy-start.1
  33.3 0.5 convert_reduce_fusion.1
  33.8 1.1 copy-done.1
  34.9 0.9 copy.13
  35.8 0.0 copy-start.2
  35.8 1.3 copy-done.2
  37.1 1.5 %fusion.8 = f32[64,4096]{1,0:T(8,128)} fusion(bf16[256,4096]{1,0:T(8,128)(2,1)S(1)} %bitcast.21, f32[64,256]{1,0:T(8,128)S(1)} %get-tuple-element.20), kind=kOutput, calls=%fused_computation.26 | convolution fusion | flops 134250496 | bytes 3211264 | tf_op jit(solution)/shard_map/dot_general | solution.py:27
  38.6 1.6 %subtract_dynamic-update-slice_fusion = f32[64,4096]{1,0:T(8,128)} fusion(f32[64,4096]{1,0:T(8,128)} %fusion.8, s32[]{:T(128)S(6)} %select_n.9, f32[4,4096]{1,0:T(4,128)S(1)} %bitcast.24, f32[4096]{0:T(1024)S(1)} %bitcast.25), kind=kLoop, calls=%fused_computation.20 | loop fusion | flops 32768 | bytes 212996 | tf_op jit(solution)/shard_map/dynamic_update_slice | solution.py:30
  40.1 70.1 %all-reduce.1 = bf16[64,4096]{1,0:T(8,128)(2,1)S(1)} all-reduce(f32[64,4096]{1,0:T(8,128)} %subtract_dynamic-update-slice_fusion), channel_id=1, replica_groups=mesh['grp'=2,'lat'=16] {'lat'}, use_global_device_ids=true, to_apply=%region_0.0 | all-reduce | flops 262144 | bytes 1572864 | tf_op jit(solution)/shard_map/psum | solution.py:31
  110.2 2.9 %convert_reduce_fusion.2 = (f32[256]{0:T(256)}, bf16[64,256]{1,0:T(8,128)(2,1)S(1)}) fusion(f32[256]{0:T(256)S(1)} %broadcast_multiply_fusion.2, bf16[64,4096]{1,0:T(8,128)(2,1)S(1)} %all-reduce.1, bf16[256,4096]{1,0:T(8,128)(2,1)} %bitcast.22, f32[64,256]{1,0:T(8,128)S(1)} %get-tuple-element.20), kind=kOutput, calls=%fused_computation.19 | convolution fusion | flops 134332160 | bytes 2721792 | tf_op jit(solution)/shard_map/dot_general | solution.py:38
  113.1 0.1 convert_reduce_fusion
  113.3 0.6 mul.82
  113.9 0.7 reshape.48
  114.6 2.0 %fusion = bf16[4096,256]{0,1:T(8,128)(2,1)} fusion(bf16[64,256]{1,0:T(8,128)(2,1)S(1)} %get-tuple-element.18, bf16[64,4096]{1,0:T(8,128)(2,1)S(1)} %reshape.51), kind=kOutput, calls=%fused_computation.4 | convolution fusion | flops 135266304 | bytes 2654208 | tf_op jit(solution)/shard_map/dot_general | solution.py:43
  116.6 4.1 %copy.12 = bf16[4096,256]{1,0:T(8,128)(2,1)} copy(bf16[4096,256]{0,1:T(8,128)(2,1)} %fusion) | data formatting | bytes 4194304
  120.7 2.7 %convolution_multiply_fusion = f32[256,4096]{1,0:T(8,128)} fusion(bf16[64,4096]{1,0:T(8,128)(2,1)S(1)} %all-reduce.1, f32[64,256]{1,0:T(8,128)S(1)} %get-tuple-element.20), kind=kOutput, calls=%fused_computation | convolution fusion | flops 135299072 | bytes 4784128 | tf_op jit(solution)/shard_map/dot_general | solution.py:35
  123.3 6.6 %mul.74 = f32[256,2,2048]{2,1,0:T(2,128)} reshape(f32[256,4096]{1,0:T(8,128)} %convolution_multiply_fusion) | data formatting | bytes 8388608 | tf_op jit(solution)/shard_map/mul | solution.py:50
  129.9 6.7 %fusion.4 = bf16[256,2,2048]{2,1,0:T(2,128)(2,1)} fusion(f32[256,2,2048]{2,1,0:T(2,128)} %mul.74, bf16[256,2,2048]{2,1,0:T(2,128)(2,1)} %param.8, f32[256]{0:T(256)S(1)} %broadcast_multiply_fusion.1, f32[256,2]{1,0:T(8,128)S(1)} %get-tuple-element.15), kind=kLoop, calls=%fused_computation.8 | loop fusion | flops 5242880 | bytes 8391680 | tf_op jit(solution)/shard_map/convert_element_type | solution.py:52
  (5 shorter events, 0.1 us)
Async XLA Ops:
  0.6 1.6 %copy-start = (bf16[2,2048,256]{2,1,0:T(8,128)(2,1)S(1)}, bf16[2,2048,256]{2,1,0:T(8,128)(2,1)}, u32[]{:S(2)}) copy-start(bf16[2,2048,256]{2,1,0:T(8,128)(2,1)} %param.6) | copy-start | bytes 6291460
  4.5 28.8 %copy-start.3 = (f32[256]{0:T(256)S(1)}, f32[256]{0:T(256)}, u32[]{:S(2)}) copy-start(f32[256]{0:T(256)} %param.7) | copy-start | bytes 3076
  33.3 1.6 %copy-start.1 = (bf16[256,2,2048]{2,1,0:T(2,128)(2,1)S(1)}, bf16[256,2,2048]{2,1,0:T(2,128)(2,1)}, u32[]{:S(2)}) copy-start(bf16[256,2,2048]{2,1,0:T(2,128)(2,1)} %param.8) | copy-start | bytes 6291460
  35.8 1.3 copy-start.2
where the time goes:
time: 137 us
  blocking collectives  94.7 us (69%)
  local copies, waits for them, and re-layouts  18.5 us (14%)
  other arithmetic  13.1 us (10%)
  matrix products  9.56 us (7%)
    psum x1, blocking collectives, body(): summed = lax.psum(term, 'lat')  70.1 us
    all_gather x1, blocking collectives, body(): gathered = lax.all_gather(flat_rows, 'lat', axis=0, tiled=True)  24.6 us
    unnamed x14, local copies, waits for them, and re-layouts  10.6 us
    convert_element_type x1, other arithmetic, body(): grad_dec = (factor * dec_total.reshape(lat_dev, layers, width) + sparsity...  6.65 us
    mul x1, local copies, waits for them, and re-layouts, body(): factor * dec_total.reshape(lat_dev, layers, width)  6.57 us
    reduce_sum x1, other arithmetic, body(): row_sq = jnp.sum(dec_wide * dec_wide, axis=2)  3.84 us
    dot_general x1, matrix products, body(): lax.dot_general(all_residual, flat_dec, (((1,), (1,)), ((), ())), preferr...  2.94 us

commit v1 on v0

--- a/solution.py
+++ b/solution.py
@@ -28,7 +28,7 @@
     own_term = lax.dynamic_slice_in_dim(term, own_start, tok_dev, 0)
     own_term = own_term + flat_bias - flat_rows.astype(jnp.float32)
     term = lax.dynamic_update_slice_in_dim(term, own_term, own_start, 0)
-    summed = lax.psum(term, "lat")
+    summed = jnp.sum(lax.all_gather(term, "lat"), axis=0)
     all_residual = summed.astype(jnp.bfloat16)
     own_residual = lax.dynamic_slice_in_dim(all_residual, own_start, tok_dev, 0)
     grad_dec_bias = factor * jnp.sum(all_residual.astype(jnp.float32), axis=0)

time: 137 us -> 204 us (1.49)
  waiting for transfers between devices: 0 us -> 120 us
  blocking collectives: 94.7 us -> 24.6 us
  between operations: 0.74 us -> 14.2 us
  other arithmetic: 13.1 us -> 20 us
  matrix products: 9.56 us -> 7.01 us
    all_gather x0 -> x1, waiting for transfers between devices: none -> 120 us  [body(): summed = jnp.sum(lax.all_gather(term, 'lat'), axis=0)]
    psum x1 -> x0, blocking collectives: 70.1 us -> none  [body(): summed = lax.psum(term, 'lat')]
    reduce_sum x0 -> x1, other arithmetic: none -> 6.89 us  [body(): summed = jnp.sum(lax.all_gather(term, 'lat'), axis=0)]
    unnamed x14 -> x19, local copies, waits for them, and re-layouts: 10.6 us -> 9.96 us
  transfers between devices with their start and end apart: 0 -> 1, of which waited for: 0 -> 1; matrix products, arithmetic and copies ran while one was open for 0% -> 2% of each run, Pallas kernels for 0% -> 0%
where the time goes in v1:
time: 204 us
  waiting for transfers between devices  120 us (59%)
  blocking collectives  24.6 us (12%)
  other arithmetic  20 us (10%)
  local copies, waits for them, and re-layouts  17.8 us (9%)
  between operations  14.2 us (7%)
  matrix products  7.01 us (3%)
    all_gather x1, waiting for transfers between devices, body(): summed = jnp.sum(lax.all_gather(term, 'lat'), axis=0)  120 us
    all_gather x1, blocking collectives, body(): gathered = lax.all_gather(flat_rows, 'lat', axis=0, tiled=True)  24.6 us
    unnamed x19, local copies, waits for them, and re-layouts  9.96 us
    reduce_sum x1, other arithmetic, body(): summed = jnp.sum(lax.all_gather(term, 'lat'), axis=0)  6.89 us
    convert_element_type x1, other arithmetic, body(): grad_dec = (factor * dec_total.reshape(lat_dev, layers, width) + sparsity...  6.65 us
    mul x1, local copies, waits for them, and re-layouts, body(): factor * dec_total.reshape(lat_dev, layers, width)  6.57 us
  transfers between devices with their start and end apart: 1, of which 1 were waited for; matrix products, arithmetic and copies ran while one was open for 2% of the time, Pallas kernels for 0%

profile of v1, /device:TPU:0, one launch (start us, length us, event | category | flops | bytes accessed | tf_op | source)
XLA Modules:
  0.0 203.5 jit_solution(15439471231119686037)
XLA Ops:
  7.2 0.0 copy-start
  7.2 0.0 all-gather.3.cloned.1.call-start
  7.2 0.9 reshape.52
  8.2 0.8 convert_bitcast_fusion
  8.9 24.6 %all-gather = bf16[16,4,4096]{2,1,0:T(4,128)(2,1)S(1)} all-gather(bf16[1,4,4096]{2,1,0:T(4,128)(2,1)S(1)} %reshape.52), channel_id=1, replica_groups=mesh['grp'=2,'lat'=16] {'lat'}, dimensions={0}, use_global_device_ids=true | all-gather | bytes 557056 | tf_op jit(solution)/shard_map/all_gather | solution.py:20
  33.6 0.1 reshape.53
  33.7 0.0 copy-start.5
  33.7 2.5 %copy.13 = bf16[32,8,2,2048]{3,1,2,0:T(8,128)(2,1)S(1)} copy(bf16[32,8,2,2048]{3,2,1,0:T(2,128)(2,1)} %bitcast.23) | data formatting | bytes 4194304
  36.2 0.0 copy-done
  36.2 0.0 copy-start.1
  36.2 0.0 copy-done.5
  36.2 0.5 convert_reduce_fusion.1
  36.7 0.0 copy-start.4
  36.7 0.5 fusion.8
  37.2 0.3 copy-done.1
  37.5 0.0 copy-start.3
  37.5 1.0 copy-done.3
  38.5 1.0 copy.16
  39.5 0.0 copy-done.4
  39.6 1.6 bitcast_dynamic-update-slice_fusion
  41.1 0.0 all-gather.3.cloned.1.call-update
  41.1 3.8 %fusion.1 = f32[256,2]{1,0:T(8,128)S(1)} fusion(bf16[256,2,2048]{2,1,0:T(2,128)(2,1)} %param.8), kind=kLoop, calls=%fused_computation.5 | loop fusion | flops 3145216 | bytes 2099200 | tf_op jit(solution)/shard_map/reduce_sum | solution.py:24
  45.0 0.1 add_rsqrt_fusion
  45.1 119.9 %all-gather.3.cloned.1.call-done = f32[16,64,4096]{2,1,0:T(8,128)} async-done(((f32[1,64,4096]{2,1,0:T(8,128)}), f32[16,64,4096]{2,1,0:T(8,128)}) %all-gather.3.cloned.1.call-update) | async-done | bytes 16777232 | tf_op jit(solution)/shard_map/all_gather | solution.py:31
  165.0 6.9 %reduce_sum.54 = bf16[64,4096]{1,0:T(8,128)(2,1)S(1)} reduce(f32[16,64,4096]{2,1,0:T(8,128)} %all-gather.3.cloned.1.call-done, f32[]{:T(128)} %constant.7.clone.1), dimensions={0}, to_apply=%region_0.0 | reduce | flops 3932160 | bytes 17301508 | tf_op jit(solution)/shard_map/reduce_sum | solution.py:31
  171.9 0.0 copy-start.2
  171.9 2.7 %convolution_multiply_fusion = f32[256,4096]{1,0:T(8,128)} fusion(bf16[64,4096]{1,0:T(8,128)(2,1)S(1)} %reduce_sum.54, f32[64,256]{1,0:T(8,128)S(1)} %get-tuple-element.20), kind=kOutput, calls=%fused_computation | convolution fusion | flops 135299072 | bytes 4784128 | tf_op jit(solution)/shard_map/dot_general | solution.py:35
  174.6 0.1 convert_reduce_fusion
  174.7 0.0 copy-done.2
  174.7 1.3 convert_reduce_fusion.2
  176.0 2.0 %fusion = bf16[4096,256]{0,1:T(8,128)(2,1)} fusion(bf16[64,256]{1,0:T(8,128)(2,1)S(1)} %get-tuple-element.18, bf16[64,4096]{1,0:T(8,128)(2,1)S(1)} %reshape.53), kind=kOutput, calls=%fused_computation.4 | convolution fusion | flops 135266304 | bytes 2654208 | tf_op jit(solution)/shard_map/dot_general | solution.py:43
  178.1 4.1 %copy.12 = bf16[4096,256]{1,0:T(8,128)(2,1)} copy(bf16[4096,256]{0,1:T(8,128)(2,1)} %fusion) | data formatting | bytes 4194304
  182.1 6.6 %mul.74 = f32[256,2,2048]{2,1,0:T(2,128)} reshape(f32[256,4096]{1,0:T(8,128)} %convolution_multiply_fusion) | data formatting | bytes 8388608 | tf_op jit(solution)/shard_map/mul | solution.py:50
  188.7 0.7 reshape.50
  189.4 0.6 mul.82
  190.0 6.7 %fusion.4 = bf16[256,2,2048]{2,1,0:T(2,128)(2,1)} fusion(f32[256,2,2048]{2,1,0:T(2,128)} %mul.74, bf16[256,2,2048]{2,1,0:T(2,128)(2,1)} %param.8, f32[256]{0:T(256)S(1)} %broadcast_multiply_fusion.1, f32[256,2]{1,0:T(8,128)S(1)} %get-tuple-element.15), kind=kLoop, calls=%fused_computation.8 | loop fusion | flops 5242880 | bytes 8391680 | tf_op jit(solution)/shard_map/convert_element_type | solution.py:52
  (6 shorter events, 0.1 us)
Async XLA Ops:
  7.2 29.0 %copy-start = (bf16[2,2048,256]{2,1,0:T(8,128)(2,1)S(1)}, bf16[2,2048,256]{2,1,0:T(8,128)(2,1)}, u32[]{:S(2)}) copy-start(bf16[2,2048,256]{2,1,0:T(8,128)(2,1)} %param.6) | copy-start | bytes 6291460
  7.2 157.8 %all-gather.3.cloned.1.call-start = ((), (), s32[]{:S(2)}) async-start(), calls=%async_computation | async-start | bytes 17825792 | tf_op jit(solution)/shard_map/all_gather | solution.py:31
  33.7 2.5 %copy-start.5 = (f32[256]{0:T(256)S(1)}, f32[256]{0:T(256)}, u32[]{:S(2)}) copy-start(f32[256]{0:T(256)} %param.7) | copy-start | bytes 3076
  36.2 1.3 copy-start.1
  36.7 2.8 %copy-start.4 = (f32[2,2048]{1,0:T(2,128)S(1)}, f32[2,2048]{1,0:T(2,128)}, u32[]{:S(2)}) copy-start(f32[2,2048]{1,0:T(2,128)} %param.9) | copy-start | bytes 49156
  37.5 1.0 copy-start.3
  171.9 2.8 %copy-start.2 = (bf16[32,8,2,2048]{3,1,2,0:T(8,128)(2,1)S(1)}, bf16[32,8,2,2048]{3,1,2,0:T(8,128)(2,1)}, u32[]{:S(2)}) copy-start(bf16[32,8,2,2048]{3,1,2,0:T(8,128)(2,1)} %copy-done.1) | copy-start | bytes 6291460
Sparse Core Ops, SparseCore 0:
  41.3 123.6 all-gather.2
